TPU v7x, 32 devices: a whole 2x2x4 slice. The times are simulated.
32 devices in a mesh: img: 4 (over x, core), tp: 8 (over z, y).
Axes of the slice: x: 2, y: 2, z: 4, core: 2. Of those that a mesh axis runs over, the one named last changes fastest.
Arguments:
- patch_tokens: bfloat16 [4096, 1024], P(('img', 'tp')), may hold values from -12 to 12
- norm_gain: float32 [1024], replicated, may hold values from 0.1 to 1.9
- norm_bias: float32 [1024], replicated, may hold values from -3 to 3
- up_weight: bfloat16 [1024, 8192], P('img', 'tp'), may hold values from -0.1875 to 0.1875
- up_bias: float32 [8192], P('tp'), may hold values from -3 to 3
- down_weight: bfloat16 [8192, 4096], P('tp', 'img'), may hold values from -0.125 to 0.125
- down_bias: float32 [4096], replicated, may hold values from -3 to 3
Outputs:
- projected: bfloat16 [4096, 4096], P(('img', 'tp'))
All inputs are finite; a program needn't handle non-finite values.
Results may differ from a plain program's by a relative error of at most 0.014.
Values may be sent and summed in bfloat16 or wider, within the bound.
A program may use at most 128 MiB of HBM per device.

v0:
```python
import jax
import jax.numpy as jnp
from jax import lax
from jax.sharding import PartitionSpec as P


def on_device(patch_tokens, norm_gain, norm_bias, up_weight, up_bias, down_weight, down_bias):
    values = lax.all_gather(patch_tokens, "tp", axis=0, tiled=True).astype(jnp.float32)
    center = jnp.mean(values, axis=1, keepdims=True)
    spread = jnp.mean((values - center) ** 2, axis=1, keepdims=True)
    gathered = ((values - center) * lax.rsqrt(spread + 1e-05) * norm_gain + norm_bias).astype(
        jnp.bfloat16
    )
    summed = jnp.dot(
        gathered,
        lax.all_gather(up_weight, "img", axis=0, tiled=True),
        preferred_element_type=jnp.float32,
    )
    hidden = jax.nn.gelu(summed + up_bias).astype(jnp.bfloat16)
    down_full = lax.all_gather(down_weight, "img", axis=1, tiled=True)
    total = lax.psum_scatter(
        jnp.dot(hidden, down_full, preferred_element_type=jnp.float32).astype(jnp.bfloat16),
        "tp",
        scatter_dimension=0,
        tiled=True,
    ).astype(jnp.float32)
    return (total + down_bias).astype(jnp.bfloat16)


def solution(mesh):
    return jax.shard_map(
        on_device,
        mesh=mesh,
        in_specs=(P(("img", "tp"), None), P(), P(), P("img", "tp"), P("tp"), P("tp", "img"), P()),
        out_specs=P(("img", "tp"), None),
        check_vma=False,
    )
```

profile of v0, /device:TPU:0, one launch (start us, length us, event | category | flops | bytes accessed | tf_op | source)
XLA Modules:
  0.0 318.9 jit_solution(16244446734320534299)
XLA Ops:
  6.5 0.0 copy-start.2
  6.5 0.0 copy-start.3
  6.5 0.0 copy-start.4
  6.5 0.0 all-gather.4.cloned.1.call-start
  6.5 0.7 all-gather.4.cloned.1.call-update
  7.3 0.0 all-gather.6.cloned.1.call-start
  7.3 0.7 all-gather.6.cloned.1.call-update
  8.0 0.0 all-gather.8.cloned.1.call-start
  8.1 0.7 all-gather.8.cloned.1.call-update
  8.7 0.0 reduce-scatter.2.cloned.1.call-start
  8.8 52.5 %all-gather.4.cloned.1.call-done = bf16[1024,1024]{1,0:T(8,128)(2,1)} async-done(((bf16[128,1024]{1,0:T(8,128)(2,1)}), bf16[1024,1024]{1,0:T(8,128)(2,1)}) %all-gather.4.cloned.1.call-update) | async-done | bytes 2097168 | tf_op jit(solution)/shard_map/all_gather | solution.py:8
  61.3 0.0 copy-start
  61.3 2.1 convert_reduce_fusion
  63.4 2.3 fusion.2
  65.7 18.3 %all-gather.6.cloned.1.call-done = bf16[1024,1024]{1,0:T(8,128)(2,1)} async-done(((bf16[256,1024]{1,0:T(8,128)(2,1)}), bf16[1024,1024]{1,0:T(8,128)(2,1)}) %all-gather.6.cloned.1.call-update) | async-done | bytes 2097168 | tf_op jit(solution)/shard_map/all_gather | solution.py:16
  84.0 59.9 %all-gather.8.cloned.1.call-done = bf16[1024,4096]{1,0:T(8,128)(2,1)} async-done(((bf16[1024,1024]{1,0:T(8,128)(2,1)}), bf16[1024,4096]{1,0:T(8,128)(2,1)}) %all-gather.8.cloned.1.call-update) | async-done | bytes 8388624 | tf_op jit(solution)/shard_map/all_gather | solution.py:20
  143.9 0.0 copy-done.2
  143.9 0.0 copy-done.3
  143.9 0.0 copy-done.4
  143.9 0.0 copy-done
  143.9 18.4 %convolution_convert_fusion = bf16[1024,4096]{1,0:T(8,128)(2,1)} fusion(bf16[1024,4096]{1,0:T(8,128)(2,1)} %all-gather.8.cloned.1.call-done, bf16[1024,1024]{1,0:T(8,128)(2,1)} %all-gather.6.cloned.1.call-done, bf16[1024,1024]{1,0:T(8,128)(2,1)S(1)} %copy-done, f32[1024]{0:T(1024)S(1)} %copy-done.2, f32[1024]{0:T(1024)S(1)} %copy-done.3, ...), kind=kOutput, calls=%fused_computation | convolution fusion | flops 10758389760 | bytes 20992000 | tf_op jit(solution)/shard_map/dot_general | solution.py:22
  162.3 0.0 copy-start.1
  162.3 0.0 reduce-scatter.2.cloned.1.call-update
  162.3 147.6 %reduce-scatter.2.cloned.1.call-done = bf16[128,4096]{1,0:T(8,128)(2,1)} async-done(((bf16[1024,4096]{1,0:T(8,128)(2,1)}), bf16[128,4096]{1,0:T(8,128)(2,1)}) %reduce-scatter.2.cloned.1.call-update) | async-done | bytes 1048592 | tf_op jit(solution)/shard_map/reduce_scatter | solution.py:21
  309.9 0.0 copy-done.1
  310.0 2.4 add_convert_fusion
  (2 shorter events, 0.0 us)
Async XLA Ops:
  6.5 137.3 %copy-start.2 = (f32[1024]{0:T(1024)S(1)}, f32[1024]{0:T(1024)}, u32[]{:S(2)}) copy-start(f32[1024]{0:T(1024)} %param.11) | copy-start | bytes 12292
  6.5 137.3 %copy-start.3 = (f32[1024]{0:T(1024)S(1)}, f32[1024]{0:T(1024)}, u32[]{:S(2)}) copy-start(f32[1024]{0:T(1024)} %param.9) | copy-start | bytes 12292
  6.5 137.3 %copy-start.4 = (f32[1024]{0:T(1024)S(1)}, f32[1024]{0:T(1024)}, u32[]{:S(2)}) copy-start(f32[1024]{0:T(1024)} %param.8) | copy-start | bytes 12292
  6.5 54.8 %all-gather.4.cloned.1.call-start = ((), (), s32[]{:S(2)}) async-start(), calls=%async_computation.1 | async-start | bytes 2359296 | tf_op jit(solution)/shard_map/all_gather | solution.py:8
  7.3 76.7 %all-gather.6.cloned.1.call-start = ((), (), s32[]{:S(2)}) async-start(), calls=%async_computation.2 | async-start | bytes 2621440 | tf_op jit(solution)/shard_map/all_gather | solution.py:16
  8.0 135.8 %all-gather.8.cloned.1.call-start = ((), (), s32[]{:S(2)}) async-start(), calls=%async_computation.3 | async-start | bytes 10485760 | tf_op jit(solution)/shard_map/all_gather | solution.py:20
  8.7 301.2 %reduce-scatter.2.cloned.1.call-start = ((), (), s32[]{:S(2)}) async-start(), calls=%async_computation.4 | async-start | bytes 9437184 | tf_op jit(solution)/shard_map/reduce_scatter | solution.py:21
  61.3 82.6 %copy-start = (bf16[1024,1024]{1,0:T(8,128)(2,1)S(1)}, bf16[1024,1024]{1,0:T(8,128)(2,1)}, u32[]{:S(2)}) copy-start(bf16[1024,1024]{1,0:T(8,128)(2,1)} %all-gather.4.cloned.1.call-done) | copy-start | bytes 6291460
  162.3 147.7 %copy-start.1 = (f32[4096]{0:T(1024)S(1)}, f32[4096]{0:T(1024)}, u32[]{:S(2)}) copy-start(f32[4096]{0:T(1024)} %param.13) | copy-start | bytes 49156
Sparse Core Ops, SparseCore 0:
  9.5 51.7 all-gather.3
  62.9 21.0 all-gather.5
  85.6 58.2 all-gather.7
  162.4 147.4 reduce-scatter.1
where the time goes:
time: 319 us
  waiting for transfers between devices  280 us (88%)
  matrix products  18.4 us (6%)
  between operations  13.1 us (4%)
  other arithmetic  6.78 us (2%)
    reduce_scatter x1, waiting for transfers between devices, on_device(): lax.psum_scatter(jnp.dot(hidden, down_full, preferred_element_type=jnp.fl...  148 us
    all_gather x1, waiting for transfers between devices, on_device(): down_full = lax.all_gather(down_weight, 'img', axis=1, tiled=True)  59.9 us
    all_gather x1, waiting for transfers between devices, on_device(): lax.all_gather(patch_tokens, 'tp', axis=0, tiled=True).astype(jnp.float32)  52.5 us
    dot_general x1, matrix products, on_device(): jnp.dot(hidden, down_full, preferred_element_type=jnp.float32)  18.4 us
    all_gather x1, waiting for transfers between devices, on_device(): lax.all_gather(up_weight, 'img', axis=0, tiled=True)  18.3 us
  transfers between devices with their start and end apart: 4, of which 4 were waited for; matrix products, arithmetic and copies ran while one was open for 1% of the time, Pallas kernels for 0%

commit v1 on v0

--- a/solution.py
+++ b/solution.py
@@ -17,7 +17,16 @@
         preferred_element_type=jnp.float32,
     )
     hidden = jax.nn.gelu(summed + up_bias).astype(jnp.bfloat16)
-    down_full = lax.all_gather(down_weight, "img", axis=1, tiled=True)
+    many = lax.psum(1, "img")
+    reply = [None] * many
+    reply[many - 1] = down_weight
+    pile = [(i, (i + 1) % many) for i in range(many)]
+    for d in range(many - 2, -1, -1):
+        reply[d] = lax.ppermute(reply[d + 1], "img", pile)
+    fresh = jnp.concatenate(reply, 1)
+    work_now = lax.axis_index("img")
+    block_last = (work_now + 1) * down_weight.shape[1]
+    down_full = jnp.roll(fresh, block_last, 1)
     total = lax.psum_scatter(
         jnp.dot(hidden, down_full, preferred_element_type=jnp.float32).astype(jnp.bfloat16),
         "tp",

time: 319 us -> 291 us (0.912)
  waiting for transfers between devices: 280 us -> 234 us
  local copies, waits for them, and re-layouts: 0.02 us -> 18.7 us
    ppermute x0 -> x3, waiting for transfers between devices: none -> 81 us  [on_device(): reply[d] = lax.ppermute(reply[d + 1], 'img', pile)]
    all_gather x1 -> x0, waiting for transfers between devices: 59.9 us -> none  [on_device(): down_full = lax.all_gather(down_weight, 'img', axis=1, tiled=True)]
    all_gather x1, waiting for transfers between devices: 52.5 us -> 2.76 us  [on_device(): lax.all_gather(patch_tokens, 'tp', axis=0, tiled=True).astype(jnp.float32)]
    all_gather x1, waiting for transfers between devices: 18.3 us -> 0.01 us  [on_device(): lax.all_gather(up_weight, 'img', axis=0, tiled=True)]
    unnamed x10 -> x23, local copies, waits for them, and re-layouts: 0.02 us -> 17.2 us
  transfers between devices with their start and end apart: 4 -> 6, of which waited for: 4 -> 5; matrix products, arithmetic and copies ran while one was open for 1% -> 8% of each run, Pallas kernels for 0% -> 0%
where the time goes in v1:
time: 291 us
  waiting for transfers between devices  234 us (80%)
  local copies, waits for them, and re-layouts  18.7 us (6%)
  matrix products  18.4 us (6%)
  between operations  13.2 us (5%)
  other arithmetic  6.63 us (2%)
    reduce_scatter x1, waiting for transfers between devices, on_device(): lax.psum_scatter(jnp.dot(hidden, down_full, preferred_element_type=jnp.fl...  150 us
    ppermute x3, waiting for transfers between devices, on_device(): reply[d] = lax.ppermute(reply[d + 1], 'img', pile)  81 us
    dot_general x1, matrix products, on_device(): jnp.dot(hidden, down_full, preferred_element_type=jnp.float32)  18.4 us
    unnamed x23, local copies, waits for them, and re-layouts  17.2 us
  transfers between devices with their start and end apart: 6, of which 5 were waited for; matrix products, arithmetic and copies ran while one was open for 8% of the time, Pallas kernels for 0%

profile of v1, /device:TPU:0, one launch (start us, length us, event | category | flops | bytes accessed | tf_op | source)
XLA Modules:
  0.0 291.2 jit_solution(256004349083801211)
XLA Ops:
  6.5 0.0 all-gather.3.cloned.1.call-start
  6.5 0.5 collective-permute-start
  7.0 0.2 all-gather.3.cloned.1.call-update
  7.3 0.0 all-gather.5.cloned.1.call-start
  7.3 25.6 %collective-permute-done = bf16[1024,1024]{1,0:T(8,128)(2,1)S(1)} collective-permute-done((bf16[1024,1024]{1,0:T(8,128)(2,1)}, bf16[1024,1024]{1,0:T(8,128)(2,1)S(1)}, u32[]{:S(2)}, u32[]{:S(2)}) %collective-permute-start) | collective-permute-done | bytes 2097184 | tf_op jit(solution)/shard_map/ppermute | solution.py:25
  32.9 0.0 copy-start.2
  32.9 0.0 collective-permute-start.1
  32.9 25.5 %collective-permute-done.1 = bf16[1024,1024]{1,0:T(8,128)(2,1)} collective-permute-done((bf16[1024,1024]{1,0:T(8,128)(2,1)S(1)}, bf16[1024,1024]{1,0:T(8,128)(2,1)}, u32[]{:S(2)}, u32[]{:S(2)}) %collective-permute-start.1) | collective-permute-done | bytes 2097184 | tf_op jit(solution)/shard_map/ppermute | solution.py:25
  58.4 0.0 collective-permute-start.2
  58.4 0.0 all-gather.5.cloned.1.call-update
  58.5 0.0 reduce-scatter.2.cloned.1.call-start
  58.5 2.8 all-gather.3.cloned.1.call-done
  61.3 1.9 convert_reduce_fusion
  63.2 2.3 fusion.7
  65.5 29.9 %collective-permute-done.2 = bf16[1024,1024]{1,0:T(8,128)(2,1)} collective-permute-done((bf16[1024,1024]{1,0:T(8,128)(2,1)}, bf16[1024,1024]{1,0:T(8,128)(2,1)}, u32[]{:S(2)}, u32[]{:S(2)}) %collective-permute-start.2) | collective-permute-done | bytes 2097184 | tf_op jit(solution)/shard_map/ppermute | solution.py:25
  95.4 3.1 %constant_dynamic-update-slice_fusion.7 = bf16[1024,8192]{1,0:T(8,128)(2,1)} fusion(bf16[1024,1024]{1,0:T(8,128)(2,1)} %collective-permute-done.2), kind=kLoop, calls=%fused_computation.38 | loop fusion | bytes 4194304
  98.5 0.0 copy-start
  98.5 3.2 %constant_dynamic-update-slice_fusion.6 = bf16[1024,8192]{1,0:T(8,128)(2,1)} fusion(bf16[1024,8192]{1,0:T(8,128)(2,1)} %constant_dynamic-update-slice_fusion.7, bf16[1024,1024]{1,0:T(8,128)(2,1)} %collective-permute-done.1), kind=kLoop, calls=%fused_computation.37 | loop fusion | bytes 4194304
  101.8 0.0 copy-done.2
  101.8 1.5 constant_dynamic-update-slice_fusion.5
  103.3 0.0 copy-done
  103.3 1.5 constant_dynamic-update-slice_fusion.4
  104.8 0.0 copy-start.3
  104.8 3.3 %constant_dynamic-update-slice_fusion.3 = bf16[1024,8192]{1,0:T(8,128)(2,1)} fusion(bf16[1024,8192]{1,0:T(8,128)(2,1)} %constant_dynamic-update-slice_fusion.4, bf16[1024,1024]{1,0:T(8,128)(2,1)} %collective-permute-done.2), kind=kLoop, calls=%fused_computation.34 | loop fusion | bytes 4194304
  108.0 3.1 %constant_dynamic-update-slice_fusion.2 = bf16[1024,8192]{1,0:T(8,128)(2,1)} fusion(bf16[1024,8192]{1,0:T(8,128)(2,1)} %constant_dynamic-update-slice_fusion.3, bf16[1024,1024]{1,0:T(8,128)(2,1)} %collective-permute-done.1), kind=kLoop, calls=%fused_computation.33 | loop fusion | bytes 4194304
  111.2 0.0 copy-done.3
  111.2 0.0 copy-start.1
  111.2 0.0 copy-start.5
  111.2 0.0 copy-start.6
  111.2 0.0 copy-start.7
  111.2 1.5 constant_dynamic-update-slice_fusion.1
  112.7 1.5 constant_dynamic-update-slice_fusion
  114.2 0.0 all-gather.5.cloned.1.call-done
  114.2 0.0 copy-done.1
  114.2 0.0 copy-done.5
  114.2 0.0 copy-done.6
  114.2 0.0 copy-done.7
  114.2 18.4 %fusion.2 = bf16[1024,4096]{1,0:T(8,128)(2,1)} fusion(bf16[1024,8192]{1,0:T(8,128)(2,1)} %constant_dynamic-update-slice_fusion, s32[]{:T(128)S(6)} %select_n.14, f32[1024]{0:T(1024)S(1)} %copy-done.5, bf16[1024,1024]{1,0:T(8,128)(2,1)} %all-gather.5.cloned.1.call-done, bf16[1024,1024]{1,0:T(8,128)(2,1)S(1)} %copy-done.1, f32[1024]{0:T(1024)S(1)} %copy-done.6, ...), kind=kOutput, calls=%fused_computation.2 | convolution fusion | flops 10758389760 | bytes 20992004 | tf_op jit(solution)/shard_map/dot_general | solution.py:31
  132.6 0.0 copy-start.4
  132.6 0.0 reduce-scatter.2.cloned.1.call-update
  132.6 149.6 %reduce-scatter.2.cloned.1.call-done = bf16[128,4096]{1,0:T(8,128)(2,1)} async-done(((bf16[1024,4096]{1,0:T(8,128)(2,1)}), bf16[128,4096]{1,0:T(8,128)(2,1)}) %reduce-scatter.2.cloned.1.call-update) | async-done | bytes 1048592 | tf_op jit(solution)/shard_map/reduce_scatter | solution.py:30
  282.3 0.0 copy-done.4
  282.3 2.4 add_convert_fusion
  (2 shorter events, 0.0 us)
Async XLA Ops:
  6.5 54.8 %all-gather.3.cloned.1.call-start = ((), (), s32[]{:S(2)}) async-start(), calls=%async_computation.1 | async-start | bytes 2359296 | tf_op jit(solution)/shard_map/all_gather | solution.py:8
  6.5 26.3 %collective-permute-start = (bf16[1024,1024]{1,0:T(8,128)(2,1)}, bf16[1024,1024]{1,0:T(8,128)(2,1)S(1)}, u32[]{:S(2)}, u32[]{:S(2)}) collective-permute-start(bf16[1024,1024]{1,0:T(8,128)(2,1)} %param.12), channel_id=1, source_target_pairs={{0,8},{8,16},{16,24},{24,0},{1,9},{9,17},{17,25},{25,1},{2,10},{10... | collective-permute-start | bytes 6291464 | tf_op jit(solution)/shard_map/ppermute | solution.py:25
  7.3 106.9 %all-gather.5.cloned.1.call-start = ((), (), s32[]{:S(2)}) async-start(), calls=%async_computation.2 | async-start | bytes 2621440 | tf_op jit(solution)/shard_map/all_gather | solution.py:16
  32.9 68.9 %copy-start.2 = (bf16[1024,1024]{1,0:T(8,128)(2,1)}, bf16[1024,1024]{1,0:T(8,128)(2,1)S(1)}, u32[]{:S(2)}) copy-start(bf16[1024,1024]{1,0:T(8,128)(2,1)S(1)} %collective-permute-done) | copy-start | bytes 6291460
  32.9 25.6 %collective-permute-start.1 = (bf16[1024,1024]{1,0:T(8,128)(2,1)S(1)}, bf16[1024,1024]{1,0:T(8,128)(2,1)}, u32[]{:S(2)}, u32[]{:S(2)}) collective-permute-start(bf16[1024,1024]{1,0:T(8,128)(2,1)S(1)} %collective-permute-done), channel_id=1, source_target_pairs={{0,8},{8,16},{16,24},{24,0},{1,9},{9,17},{17,25},{25,1},{2,10},{10... | collective-permute-start | bytes 6291464 | tf_op jit(solution)/shard_map/ppermute | solution.py:25
  58.4 37.0 %collective-permute-start.2 = (bf16[1024,1024]{1,0:T(8,128)(2,1)}, bf16[1024,1024]{1,0:T(8,128)(2,1)}, u32[]{:S(2)}, u32[]{:S(2)}) collective-permute-start(bf16[1024,1024]{1,0:T(8,128)(2,1)} %collective-permute-done.1), channel_id=1, source_target_pairs={{0,8},{8,16},{16,24},{24,0},{1,9},{9,17},{17,25},{25,1},{2,10},{10... | collective-permute-start | bytes 6291464 | tf_op jit(solution)/shard_map/ppermute | solution.py:25
  58.5 223.8 %reduce-scatter.2.cloned.1.call-start = ((), (), s32[]{:S(2)}) async-start(), calls=%async_computation.3 | async-start | bytes 9437184 | tf_op jit(solution)/shard_map/reduce_scatter | solution.py:30
  98.5 4.7 %copy-start = (bf16[1024,1024]{1,0:T(8,128)(2,1)S(1)}, bf16[1024,1024]{1,0:T(8,128)(2,1)}, u32[]{:S(2)}) copy-start(bf16[1024,1024]{1,0:T(8,128)(2,1)} %param.12) | copy-start | bytes 6291460
  104.8 6.4 %copy-start.3 = (bf16[1024,1024]{1,0:T(8,128)(2,1)S(1)}, bf16[1024,1024]{1,0:T(8,128)(2,1)}, u32[]{:S(2)}) copy-start(bf16[1024,1024]{1,0:T(8,128)(2,1)} %copy-done.2) | copy-start | bytes 6291460
  111.2 3.0 %copy-start.1 = (bf16[1024,1024]{1,0:T(8,128)(2,1)S(1)}, bf16[1024,1024]{1,0:T(8,128)(2,1)}, u32[]{:S(2)}) copy-start(bf16[1024,1024]{1,0:T(8,128)(2,1)} %all-gather.3.cloned.1.call-done) | copy-start | bytes 6291460
  111.2 3.0 %copy-start.5 = (f32[1024]{0:T(1024)S(1)}, f32[1024]{0:T(1024)}, u32[]{:S(2)}) copy-start(f32[1024]{0:T(1024)} %param.11) | copy-start | bytes 12292
  111.2 3.0 %copy-start.6 = (f32[1024]{0:T(1024)S(1)}, f32[1024]{0:T(1024)}, u32[]{:S(2)}) copy-start(f32[1024]{0:T(1024)} %param.9) | copy-start | bytes 12292
  111.2 3.0 %copy-start.7 = (f32[1024]{0:T(1024)S(1)}, f32[1024]{0:T(1024)}, u32[]{:S(2)}) copy-start(f32[1024]{0:T(1024)} %param.8) | copy-start | bytes 12292
  132.6 149.7 %copy-start.4 = (f32[4096]{0:T(1024)S(1)}, f32[4096]{0:T(1024)}, u32[]{:S(2)}) copy-start(f32[4096]{0:T(1024)} %param.13) | copy-start | bytes 49156
Sparse Core Ops, SparseCore 0:
  9.5 51.7 all-gather.2
  62.9 26.8 all-gather.4
  132.7 149.4 reduce-scatter.1
